TPU v7x, 32 devices: a whole 2x2x4 slice. The times are simulated.
32 devices in a mesh: dp: 8 (over z, x), mp: 4 (over y, core).
Axes of the slice: x: 2, y: 2, z: 4, core: 2. Of those that a mesh axis runs over, the one named last changes fastest.
Arguments:
- acts: bfloat16 [6144, 4, 1984], P('dp', 'mp'), may hold values from -6 to 6
- grads: bfloat16 [6144, 4, 1984], P('dp', 'mp'), may hold values from -0.21875 to 0.21875
- error: bfloat16 [8, 4, 1984, 1984], P('dp', 'mp'), may hold values from -4 to 4
- momentum: float32 [4, 1984, 1984], P('mp', 'dp'), may hold values from -4 to 4
- q_start: float32 [4, 1984, 128], P('mp'), may hold values from -0.125 to 0.125
Outputs:
- error_next: bfloat16 [8, 4, 1984, 1984], P('dp', 'mp')
- momentum_next: float32 [4, 1984, 1984], P('mp', 'dp')
- q_next: float32 [4, 1984, 128], P('mp')
All inputs are finite; a program needn't handle non-finite values.
Results may differ from a plain program's by a relative error of at most 0.001.
Values sent between devices are 32-bit elements; how exact they have to be, the bound alone decides.
No kernel may reach another device: no remote copies, remote signals or barrier semaphores. Data moves between devices by JAX's collectives and lax.ppermute only.
A program may use at most 128 MiB of HBM per device.

v0:
```python
import jax
import jax.numpy as jnp
from jax import lax
from jax.sharding import PartitionSpec as P

D = 3968
PRECISE = lax.Precision.HIGHEST


def per_device(acts, grads, error, momentum, q_start):
    inputs = acts[:, 0, :]
    upstream = grads[:, 0, :]
    local_grad = lax.dot_general(
        inputs, upstream, (((0,), (0,)), ((), ())), preferred_element_type=jnp.float32
    )
    merged = local_grad + error[0, 0].astype(jnp.float32)
    warm_start = q_start[0]
    replicas = lax.axis_size("dp")
    owned_rows = momentum.shape[1]
    left_local = jnp.dot(merged, warm_start, precision=PRECISE)
    left_full = lax.psum(left_local, "dp")
    gram_matrix = jnp.dot(left_full.T, left_full, precision=PRECISE)
    cholesky_low = jnp.linalg.cholesky(gram_matrix)
    ortho_basis = lax.linalg.triangular_solve(
        cholesky_low, left_full, left_side=False, lower=True, transpose_a=True
    )
    basis_owned = lax.dynamic_slice_in_dim(
        ortho_basis, lax.axis_index("dp") * owned_rows, owned_rows, 0
    )
    right_local = lax.dot_general(merged, ortho_basis, (((0,), (0,)), ((), ())), precision=PRECISE)
    q_tile = lax.psum(right_local, "dp") / replicas
    norm_total = lax.psum(jnp.sum(q_tile * q_tile), "mp")
    rms_value = jnp.sqrt(norm_total / (D * D))
    decoded = jnp.dot(ortho_basis, q_tile.T, precision=PRECISE)
    error_next = (merged - decoded).astype(jnp.bfloat16)
    update = jnp.dot(basis_owned, q_tile.T, precision=PRECISE)
    momentum_next = 0.9 * momentum[0] + 0.1 * update / (rms_value + 1e-06)
    return (error_next[None, None], momentum_next[None], q_tile[None])


def solution(mesh):
    in_specs = (
        P("dp", "mp", None),
        P("dp", "mp", None),
        P("dp", "mp", None, None),
        P("mp", "dp", None),
        P("mp", None, None),
    )
    out_specs = (P("dp", "mp", None, None), P("mp", "dp", None), P("mp", None, None))
    return jax.shard_map(
        per_device, mesh=mesh, in_specs=in_specs, out_specs=out_specs, check_vma=False
    )
```

profile of v0, /device:TPU:0, one launch (start us, length us, event | category | flops | bytes accessed | tf_op | source)
XLA Modules:
  0.0 297.2 jit_solution(10708653032430564272)
XLA Ops:
  7.2 0.0 copy-start
  7.2 0.0 all-reduce.3.cloned.1.call-start
  7.2 1.8 copy-done
  9.0 9.3 %convert_add_fusion = f32[1984,1984]{1,0:T(8,128)S(1)} fusion(bf16[1,1,1984,1984]{3,2,1,0:T(8,128)(2,1)} %param.7, bf16[768,1,1984]{0,2,1:T(8,128)(2,1)S(1)} %copy-done, bf16[768,1,1984]{0,2,1:T(8,128)(2,1)} %param.5), kind=kOutput, calls=%fused_computation | convolution fusion | flops 6053961728 | bytes 29712384 | tf_op jit(solution)/shard_map/dot_general | solution.py:13
  18.4 0.0 copy-start.1
  18.4 5.6 %copy-done.1 = f32[1984,1984]{1,0:T(8,128)} copy-done((f32[1984,1984]{1,0:T(8,128)}, f32[1984,1984]{1,0:T(8,128)S(1)}, u32[]{:S(2)}) %copy-start.1) | copy-done | bytes 15745048
  24.0 15.3 %fusion.6 = f32[1984,128]{1,0:T(8,128)} fusion(f32[1984,1984]{1,0:T(8,128)S(1)} %convert_add_fusion, f32[1,1984,128]{2,1,0:T(8,128)} %param.9), kind=kOutput, calls=%fused_computation.9 | convolution fusion | flops 6046089216 | bytes 17776640 | tf_op jit(solution)/shard_map/dot_general | solution.py:20
  39.3 0.0 all-reduce.3.cloned.1.call-update
  39.3 0.2 all-reduce.5.cloned.1.call-start
  39.6 80.8 %all-reduce.3.cloned.1.call-done = f32[1984,128]{1,0:T(8,128)} async-done(((f32[1984,128]{1,0:T(8,128)}), f32[1984,128]{1,0:T(8,128)}) %all-reduce.3.cloned.1.call-update) | async-done | bytes 1015824 | tf_op jit(solution)/shard_map/psum | solution.py:21
  120.3 3.3 %fusion.20 = f32[128,128]{1,0:T(8,128)S(1)} fusion(f32[1984,128]{1,0:T(8,128)} %all-reduce.3.cloned.1.call-done), kind=kOutput, calls=%fused_computation.31 | convolution fusion | flops 390070272 | bytes 1081344 | tf_op jit(solution)/shard_map/dot_general | solution.py:22
  123.7 0.1 copy.8
  123.8 11.7 %cholesky.16 = f32[128,128]{1,0:T(8,128)S(1)} custom-call(f32[128,128]{1,0:T(8,128)S(1)} %fusion.16), custom_call_target="Cholesky" | custom-call | tf_op jit(solution)/shard_map/jit(cholesky)/cholesky | solution.py:23
  135.5 0.6 compare_reduce_fusion
  136.2 0.7 fusion.13
  136.9 9.8 %custom-call.6 = f32[1,128,128]{1,2,0:T(8,128)S(1)} custom-call(f32[1,128,128]{2,1,0:T(8,128)S(1)} %fusion.13), custom_call_target="InvertDiagBlocksLowerTriangular" | custom-call | tf_op jit(solution)/shard_map/triangular_solve | solution.py:24
  146.7 2.2 fusion.14
  148.8 0.0 copy-start.2
  148.8 1.0 copy-done.2
  149.8 29.9 %fusion.21 = f32[1984,128]{1,0:T(8,128)} fusion(f32[1984,1984]{1,0:T(8,128)} %copy-done.1, f32[1984,128]{1,0:T(8,128)S(1)} %fusion.14), kind=kOutput, calls=%fused_computation.32 | convolution fusion | flops 6046089216 | bytes 17776640 | tf_op jit(solution)/shard_map/dot_general | solution.py:30
  179.7 0.0 all-reduce.5.cloned.1.call-update
  179.7 77.0 %all-reduce.5.cloned.1.call-done = f32[1984,128]{1,0:T(8,128)} async-done(((f32[1984,128]{1,0:T(8,128)}), f32[1984,128]{1,0:T(8,128)}) %all-reduce.5.cloned.1.call-update) | async-done | bytes 1015824 | tf_op jit(solution)/shard_map/psum | solution.py:31
  256.8 3.0 multiply_bitcast_fusion
  259.7 6.5 %psum.23 = f32[]{:T(128)} all-reduce(f32[]{:T(128)} %get-tuple-element.4), channel_id=1, replica_groups=mesh['dp'=8,'mp'=4] {'mp'}, use_global_device_ids=true, to_apply=%region_5.6 | all-reduce | flops 1 | bytes 8 | tf_op jit(solution)/shard_map/psum | solution.py:32
  266.9 0.0 copy-start.3
  267.0 0.0 copy-start.4
  267.0 19.2 %fusion = bf16[1,1,1984,1984]{3,2,1,0:T(8,128)(2,1)} fusion(f32[1984,1984]{1,0:T(8,128)} %copy-done.1, f32[1984,128]{1,0:T(8,128)} %copy-done.2, f32[1984,128]{1,0:T(8,128)} %all-reduce.5.cloned.1.call-done), kind=kOutput, calls=%fused_computation.2 | convolution fusion | flops 6054215680 | bytes 25649152 | tf_op jit(solution)/shard_map/dot_general | solution.py:34
  286.1 0.0 copy-done.3
  286.1 0.0 copy-done.4
  286.1 4.2 %fusion.5 = f32[1,248,1984]{2,1,0:T(8,128)} fusion(f32[1,248,1984]{2,1,0:T(8,128)S(1)} %copy-done.4, f32[]{:T(128)S(6)} %add.32, f32[1984,128]{1,0:T(8,128)S(1)} %copy-done.3, f32[1984,128]{1,0:T(8,128)} %copy-done.2, s32[]{:T(128)S(6)} %select_n.8), kind=kOutput, calls=%fused_computation.8 | convolution fusion | flops 757983232 | bytes 5079048 | tf_op jit(solution)/shard_map/dot_general | solution.py:36
  (2 shorter events, 0.0 us)
Async XLA Ops:
  7.2 1.9 copy-start
  7.2 113.1 %all-reduce.3.cloned.1.call-start = ((), (), s32[]{:S(2)}) async-start(), calls=%async_computation | async-start | bytes 2031616 | tf_op jit(solution)/shard_map/psum | solution.py:21
  18.4 5.6 %copy-start.1 = (f32[1984,1984]{1,0:T(8,128)}, f32[1984,1984]{1,0:T(8,128)S(1)}, u32[]{:S(2)}) copy-start(f32[1984,1984]{1,0:T(8,128)S(1)} %convert_add_fusion) | copy-start | bytes 47235076
  39.3 217.4 %all-reduce.5.cloned.1.call-start = ((), (), s32[]{:S(2)}) async-start(), calls=%async_computation.1 | async-start | bytes 2031616 | tf_op jit(solution)/shard_map/psum | solution.py:31
  148.8 1.0 copy-start.2
  266.9 19.2 %copy-start.3 = (f32[1984,128]{1,0:T(8,128)S(1)}, f32[1984,128]{1,0:T(8,128)}, u32[]{:S(2)}) copy-start(f32[1984,128]{1,0:T(8,128)} %all-reduce.5.cloned.1.call-done) | copy-start | bytes 3047428
  267.0 19.2 %copy-start.4 = (f32[1,248,1984]{2,1,0:T(8,128)S(1)}, f32[1,248,1984]{2,1,0:T(8,128)}, u32[]{:S(2)}) copy-start(f32[1,248,1984]{2,1,0:T(8,128)} %param.8) | copy-start | bytes 5904388
Sparse Core Ops, SparseCore 0:
  39.4 80.8 all-reduce.2
  179.8 76.8 all-reduce.4
where the time goes:
time: 298 us; the launch traced here: 297 us
  waiting for transfers between devices  158 us (53%)
  matrix products  83.4 us (28%)
  other arithmetic  25.8 us (9%)
  between operations  14.8 us (5%)
  local copies, waits for them, and re-layouts  8.49 us (3%)
  blocking collectives  6.53 us (2%)
    psum x1, waiting for transfers between devices, per_device(): left_full = lax.psum(left_local, 'dp')  80.8 us
    psum x1, waiting for transfers between devices, per_device(): q_tile = lax.psum(right_local, 'dp') / replicas  77 us
    dot_general x1, matrix products, per_device(): lax.dot_general(merged, ortho_basis, (((0,), (0,)), ((), ())), precision=...  29.9 us
    dot_general x1, matrix products, per_device(): decoded = jnp.dot(ortho_basis, q_tile.T, precision=PRECISE)  19.2 us
    dot_general x1, matrix products, per_device(): left_local = jnp.dot(merged, warm_start, precision=PRECISE)  15.3 us
    another operation x3, other arithmetic, per_device(): cholesky_low = jnp.linalg.cholesky(gram_matrix)  12.4 us
    another operation x2, other arithmetic, per_device(): lax.linalg.triangular_solve(cholesky_low, left_full, left_side=False, low...  10.5 us
    dot_general x1, matrix products, per_device(): lax.dot_general(inputs, upstream, (((0,), (0,)), ((), ())), preferred_ele...  9.34 us
  transfers between devices with their start and end apart: 2, of which 2 were waited for; matrix products, arithmetic and copies ran while one was open for 0% of the time, Pallas kernels for 0%

commit v1 on v0

--- a/solution.py
+++ b/solution.py
@@ -18,7 +18,7 @@
     replicas = lax.axis_size("dp")
     owned_rows = momentum.shape[1]
     left_local = jnp.dot(merged, warm_start, precision=PRECISE)
-    left_full = lax.psum(left_local, "dp")
+    left_full = jnp.sum(lax.all_gather(left_local, "dp"), axis=0)
     gram_matrix = jnp.dot(left_full.T, left_full, precision=PRECISE)
     cholesky_low = jnp.linalg.cholesky(gram_matrix)
     ortho_basis = lax.linalg.triangular_solve(

time: 298 us -> 345 us (1.16)
  waiting for transfers between devices: 158 us -> 200 us
  other arithmetic: 25.8 us -> 30.6 us
    all_gather x0 -> x1, waiting for transfers between devices: none -> 124 us  [per_device(): left_full = jnp.sum(lax.all_gather(left_local, 'dp'), axis=0)]
    psum x1 -> x0, waiting for transfers between devices: 80.8 us -> none  [per_device(): left_full = lax.psum(left_local, 'dp')]
    reduce_sum x0 -> x1, other arithmetic: none -> 4.76 us  [per_device(): left_full = jnp.sum(lax.all_gather(left_local, 'dp'), axis=0)]
where the time goes in v1:
time: 345 us; the launch traced here: 344 us
  waiting for transfers between devices  200 us (58%)
  matrix products  83.4 us (24%)
  other arithmetic  30.6 us (9%)
  between operations  14.8 us (4%)
  local copies, waits for them, and re-layouts  8.49 us (2%)
  blocking collectives  6.53 us (2%)
    all_gather x1, waiting for transfers between devices, per_device(): left_full = jnp.sum(lax.all_gather(left_local, 'dp'), axis=0)  124 us
    psum x1, waiting for transfers between devices, per_device(): q_tile = lax.psum(right_local, 'dp') / replicas  76.4 us
    dot_general x1, matrix products, per_device(): lax.dot_general(merged, ortho_basis, (((0,), (0,)), ((), ())), precision=...  29.9 us
    dot_general x1, matrix products, per_device(): decoded = jnp.dot(ortho_basis, q_tile.T, precision=PRECISE)  19.2 us
    dot_general x1, matrix products, per_device(): left_local = jnp.dot(merged, warm_start, precision=PRECISE)  15.3 us
    another operation x3, other arithmetic, per_device(): cholesky_low = jnp.linalg.cholesky(gram_matrix)  12.4 us
    another operation x2, other arithmetic, per_device(): lax.linalg.triangular_solve(cholesky_low, left_full, left_side=False, low...  10.5 us
    dot_general x1, matrix products, per_device(): lax.dot_general(inputs, upstream, (((0,), (0,)), ((), ())), preferred_ele...  9.34 us
  transfers between devices with their start and end apart: 2, of which 2 were waited for; matrix products, arithmetic and copies ran while one was open for 0% of the time, Pallas kernels for 0%

profile of v1, /device:TPU:0, one launch (start us, length us, event | category | flops | bytes accessed | tf_op | source)
XLA Modules:
  0.0 344.4 jit_solution(2979810261962262247)
XLA Ops:
  7.2 0.0 copy-start
  7.2 0.0 all-gather.3.cloned.1.call-start
  7.2 1.8 copy-done
  9.0 9.3 %convert_add_fusion = f32[1984,1984]{1,0:T(8,128)S(1)} fusion(bf16[1,1,1984,1984]{3,2,1,0:T(8,128)(2,1)} %param.7, bf16[768,1,1984]{0,2,1:T(8,128)(2,1)S(1)} %copy-done, bf16[768,1,1984]{0,2,1:T(8,128)(2,1)} %param.5), kind=kOutput, calls=%fused_computation | convolution fusion | flops 6053961728 | bytes 29712384 | tf_op jit(solution)/shard_map/dot_general | solution.py:13
  18.4 0.0 copy-start.1
  18.4 5.6 %copy-done.1 = f32[1984,1984]{1,0:T(8,128)} copy-done((f32[1984,1984]{1,0:T(8,128)}, f32[1984,1984]{1,0:T(8,128)S(1)}, u32[]{:S(2)}) %copy-start.1) | copy-done | bytes 15745048
  24.0 15.3 %fusion.6 = f32[1984,128]{1,0:T(8,128)} fusion(f32[1984,1984]{1,0:T(8,128)S(1)} %convert_add_fusion, f32[1,1984,128]{2,1,0:T(8,128)} %param.9), kind=kOutput, calls=%fused_computation.9 | convolution fusion | flops 6046089216 | bytes 17776640 | tf_op jit(solution)/shard_map/dot_general | solution.py:20
  39.3 0.0 all-gather.3.cloned.1.call-update
  39.3 0.2 all-reduce.2.cloned.1.call-start
  39.6 123.8 %all-gather.3.cloned.1.call-done = f32[15872,128]{1,0:T(8,128)} async-done(((f32[1984,128]{1,0:T(8,128)}), f32[15872,128]{1,0:T(8,128)}) %all-gather.3.cloned.1.call-update) | async-done | bytes 8126480 | tf_op jit(solution)/shard_map/all_gather | solution.py:21
  163.3 4.8 %reduce_sum.18 = f32[1984,128]{1,0:T(8,128)} reduce(f32[8,1984,128]{2,1,0:T(8,128)} %bitcast.37, f32[]{:T(128)} %constant.52.clone.1), dimensions={0}, to_apply=%region_0.0 | reduce | flops 1777664 | bytes 9142276 | tf_op jit(solution)/shard_map/reduce_sum | solution.py:21
  168.1 3.3 fusion.20
  171.4 0.1 copy.8
  171.6 11.7 %cholesky.16 = f32[128,128]{1,0:T(8,128)S(1)} custom-call(f32[128,128]{1,0:T(8,128)S(1)} %fusion.16), custom_call_target="Cholesky" | custom-call | tf_op jit(solution)/shard_map/jit(cholesky)/cholesky | solution.py:23
  183.3 0.6 compare_reduce_fusion
  183.9 0.7 fusion.13
  184.6 9.8 %custom-call.6 = f32[1,128,128]{1,2,0:T(8,128)S(1)} custom-call(f32[1,128,128]{2,1,0:T(8,128)S(1)} %fusion.13), custom_call_target="InvertDiagBlocksLowerTriangular" | custom-call | tf_op jit(solution)/shard_map/triangular_solve | solution.py:24
  194.4 2.2 fusion.14
  196.6 0.0 copy-start.2
  196.6 1.0 copy-done.2
  197.6 29.9 %fusion.21 = f32[1984,128]{1,0:T(8,128)} fusion(f32[1984,1984]{1,0:T(8,128)} %copy-done.1, f32[1984,128]{1,0:T(8,128)S(1)} %fusion.14), kind=kOutput, calls=%fused_computation.32 | convolution fusion | flops 6046089216 | bytes 17776640 | tf_op jit(solution)/shard_map/dot_general | solution.py:30
  227.5 0.0 all-reduce.2.cloned.1.call-update
  227.5 76.4 %all-reduce.2.cloned.1.call-done = f32[1984,128]{1,0:T(8,128)} async-done(((f32[1984,128]{1,0:T(8,128)}), f32[1984,128]{1,0:T(8,128)}) %all-reduce.2.cloned.1.call-update) | async-done | bytes 1015824 | tf_op jit(solution)/shard_map/psum | solution.py:31
  303.9 3.0 multiply_bitcast_fusion
  306.9 6.5 %psum.15 = f32[]{:T(128)} all-reduce(f32[]{:T(128)} %get-tuple-element.4), channel_id=1, replica_groups=mesh['dp'=8,'mp'=4] {'mp'}, use_global_device_ids=true, to_apply=%region_5.6 | all-reduce | flops 1 | bytes 8 | tf_op jit(solution)/shard_map/psum | solution.py:32
  314.1 0.0 copy-start.3
  314.1 0.0 copy-start.4
  314.1 19.2 %fusion = bf16[1,1,1984,1984]{3,2,1,0:T(8,128)(2,1)} fusion(f32[1984,1984]{1,0:T(8,128)} %copy-done.1, f32[1984,128]{1,0:T(8,128)} %copy-done.2, f32[1984,128]{1,0:T(8,128)} %all-reduce.2.cloned.1.call-done), kind=kOutput, calls=%fused_computation.2 | convolution fusion | flops 6054215680 | bytes 25649152 | tf_op jit(solution)/shard_map/dot_general | solution.py:34
  333.3 0.0 copy-done.3
  333.3 0.0 copy-done.4
  333.3 4.2 %fusion.5 = f32[1,248,1984]{2,1,0:T(8,128)} fusion(f32[1,248,1984]{2,1,0:T(8,128)S(1)} %copy-done.4, f32[]{:T(128)S(6)} %add.30, f32[1984,128]{1,0:T(8,128)S(1)} %copy-done.3, f32[1984,128]{1,0:T(8,128)} %copy-done.2, s32[]{:T(128)S(6)} %select_n.8), kind=kOutput, calls=%fused_computation.8 | convolution fusion | flops 757983232 | bytes 5079048 | tf_op jit(solution)/shard_map/dot_general | solution.py:36
  (2 shorter events, 0.0 us)
Async XLA Ops:
  7.2 1.9 copy-start
  7.2 156.2 %all-gather.3.cloned.1.call-start = ((), (), s32[]{:S(2)}) async-start(), calls=%async_computation.1 | async-start | bytes 9142272 | tf_op jit(solution)/shard_map/all_gather | solution.py:21
  18.4 5.6 %copy-start.1 = (f32[1984,1984]{1,0:T(8,128)}, f32[1984,1984]{1,0:T(8,128)S(1)}, u32[]{:S(2)}) copy-start(f32[1984,1984]{1,0:T(8,128)S(1)} %convert_add_fusion) | copy-start | bytes 47235076
  39.3 264.6 %all-reduce.2.cloned.1.call-start = ((), (), s32[]{:S(2)}) async-start(), calls=%async_computation | async-start | bytes 2031616 | tf_op jit(solution)/shard_map/psum | solution.py:31
  196.6 1.0 copy-start.2
  314.1 19.2 %copy-start.3 = (f32[1984,128]{1,0:T(8,128)S(1)}, f32[1984,128]{1,0:T(8,128)}, u32[]{:S(2)}) copy-start(f32[1984,128]{1,0:T(8,128)} %all-reduce.2.cloned.1.call-done) | copy-start | bytes 3047428
  314.1 19.2 %copy-start.4 = (f32[1,248,1984]{2,1,0:T(8,128)S(1)}, f32[1,248,1984]{2,1,0:T(8,128)}, u32[]{:S(2)}) copy-start(f32[1,248,1984]{2,1,0:T(8,128)} %param.8) | copy-start | bytes 5904388
Sparse Core Ops, SparseCore 0:
  39.4 123.8 all-gather.2
  227.6 76.2 all-reduce.1
